TPU v7x, 256 devices: a whole 4x4x8 slice. The times are simulated.
256 devices in a mesh: vocab: 256 (over x, y, z, core).
Axes of the slice: x: 4, y: 4, z: 8, core: 2. Of those that a mesh axis runs over, the one named last changes fastest.
Arguments:
- hidden: bfloat16 [2, 256, 3584], P(None, 'vocab'), may hold values from -256 to 256
- head_weight: bfloat16 [3584, 196608], P(None, 'vocab'), may hold values from -1 to 1
- teacher: bfloat16 [2, 256, 196608], P(None, None, 'vocab'), may hold values from 0 to 1
Outputs:
- token_loss: float32 [2, 256], P(None, 'vocab')
- hidden_grad: bfloat16 [2, 256, 3584], P(None, 'vocab')
- head_grad: bfloat16 [3584, 196608], P(None, 'vocab')
All inputs are finite; a program needn't handle non-finite values.
Results may differ from a plain program's by a relative error of at most 0.012.
Values may be sent and summed in bfloat16 or wider, within the bound.
A program may use at most 128 MiB of HBM per device.

v0:
```python
import jax
import jax.numpy as jnp
from jax import lax
from jax.sharding import Mesh
from jax.sharding import PartitionSpec as P

VOCAB = ("vocab_0", "vocab_1", "vocab_2", "vocab_3")


def gathered_once(value, axis):
    leaves = jax.tree.leaves(value)
    order = sorted(range(len(leaves)), key=lambda k: -leaves[k].size)
    width = (1, *leaves[order[0]].shape)[-1]
    lines = [
        jnp.pad(leaves[k].reshape(-1), (0, -leaves[k].size % width)).reshape(-1, width)
        for k in order
    ]
    both, at, found = (lax.all_gather(jnp.concatenate(lines), axis), 0, {})
    for k, line in zip(order, lines):
        slab = both[:, at : at + len(line)].reshape(len(both), -1)
        found[k] = slab[:, : leaves[k].size].reshape(-1, *leaves[k].shape)
        at += len(line)
    numbers = iter(range(len(leaves)))
    return jax.tree.map(lambda _: found[next(numbers)], value)


def joined_all(value, axes, combine):
    for axis in axes:
        pieces = gathered_once(value, axis)
        value = jax.tree.map(lambda part: part[0], pieces)
        for k in range(1, lax.axis_size(axis)):
            value = combine(value, jax.tree.map(lambda part: part[k], pieces))
    return value


def combine_rows(first, second):
    first_peak, first_total, first_mass, first_cross = first
    second_peak, second_total, second_mass, second_cross = second
    joined_peak = jnp.maximum(first_peak, second_peak)
    joined_total = first_total * jnp.exp(first_peak - joined_peak) + second_total * jnp.exp(
        second_peak - joined_peak
    )
    return (joined_peak, joined_total, first_mass + second_mass, first_cross + second_cross)


def finish(logit_block, target_block):
    target_wide = target_block.astype(jnp.float32)
    teacher_mass = jnp.sum(target_wide, axis=-1)
    cross_term = jnp.sum(target_wide * logit_block, axis=-1)
    peak_logit = jnp.max(logit_block, axis=-1)
    exp_total = jnp.sum(jnp.exp(logit_block - peak_logit[..., None]), axis=-1)
    peak_logit, exp_total, teacher_mass, cross_term = joined_all(
        (peak_logit, exp_total, teacher_mass, cross_term), VOCAB, combine_rows
    )
    log_norm = peak_logit + jnp.log(exp_total)
    token_loss = teacher_mass * log_norm - cross_term
    logit_grad = (
        teacher_mass[..., None] * jnp.exp(logit_block - log_norm[..., None]) - target_wide
    ).astype(jnp.bfloat16)
    return (token_loss, logit_grad)


def shards(hidden, head_weight, teacher):
    group_count, row_count, model_width = hidden.shape
    contract = (((1,), (1,)), ((), ()))
    shard_rows = lax.all_gather(hidden, VOCAB, axis=1, tiled=True)
    logits = jnp.einsum("crd,dv->crv", shard_rows, head_weight, preferred_element_type=jnp.float32)
    token_loss, logit_grad = finish(logits, teacher)
    row_total = lax.axis_size(VOCAB) * (group_count * row_count)
    per_group = row_total // group_count
    owner_count = per_group // row_count
    grad_block = logit_grad
    grad_block = (
        grad_block.reshape(group_count, owner_count, row_count, -1)
        .transpose(1, 0, 2, 3)
        .reshape(row_total, -1)
    )
    summed = lax.psum_scatter(
        lax.dot_general(grad_block, head_weight, contract, preferred_element_type=jnp.float32),
        VOCAB,
        scatter_dimension=0,
        tiled=True,
    )
    hidden_grad = summed.reshape(group_count, row_count, model_width).astype(jnp.bfloat16)
    weight_grad = jnp.zeros((model_width, head_weight.shape[1]), jnp.bfloat16)
    for group_index in range(group_count):
        product_term = lax.dot_general(
            shard_rows[group_index],
            logit_grad[group_index],
            (((0,), (0,)), ((), ())),
            preferred_element_type=jnp.float32,
        )
        weight_grad = (weight_grad.astype(jnp.float32) + product_term).astype(jnp.bfloat16)
    own_loss = lax.dynamic_slice_in_dim(token_loss, lax.axis_index(VOCAB) * row_count, row_count, 1)
    return (own_loss, hidden_grad, weight_grad)


def solution(mesh):
    split = Mesh(mesh.devices.reshape(4, 4, 8, 2), ("vocab_0", "vocab_1", "vocab_2", "vocab_3"))
    return jax.shard_map(
        shards,
        mesh=split,
        in_specs=(P(None, VOCAB, None), P(None, VOCAB), P(None, None, VOCAB)),
        out_specs=(P(None, VOCAB), P(None, VOCAB, None), P(None, VOCAB)),
        check_vma=False,
    )
```

profile of v0, /device:TPU:0, one launch (start us, length us, event | category | flops | bytes accessed | tf_op | source)
XLA Modules:
  0.0 362.5 jit_solution(12112623471678827758)
XLA Ops:
  7.2 0.0 all-gather.6.cloned.1.call-start
  7.2 0.7 all-gather.6.cloned.1.call-update
  7.9 0.0 copy-start
  7.9 120.6 %all-gather.6.cloned.1.call-done = bf16[2,256,3584]{2,0,1:T(2,128)(2,1)} async-done(((bf16[2,1,3584]{2,0,1:T(2,128)(2,1)}), bf16[2,256,3584]{2,0,1:T(2,128)(2,1)}) %all-gather.6.cloned.1.call-update) | async-done | bytes 3670032 | tf_op jit(solution)/shard_map/all_gather | solution.py:66
  128.5 6.8 %fusion.76 = (f32[2,256]{1,0:T(2,128)S(1)}, f32[2,256,768]{2,1,0:T(8,128)S(1)}) fusion(bf16[3584,768]{1,0:T(8,128)(2,1)} %param.4, bf16[2,256,3584]{2,0,1:T(2,128)(2,1)} %all-gather.6.cloned.1.call-done), kind=kOutput, calls=%fused_computation.155 | convolution fusion | flops 2818964992 | bytes 10749952 | tf_op jit(solution)/shard_map/crd,dv->crv/dot_general | solution.py:67
  135.2 0.0 copy-done
  135.2 0.7 exponential_reduce_fusion
  136.0 11.9 %all-gather = f32[32,256]{1,0:T(8,128)S(1)} all-gather(f32[8,256]{1,0:T(8,128)S(1)} %pad_maximum_fusion), channel_id=2, replica_groups=mesh['vocab_0'=4,'vocab_1'=4,'vocab_2'=8,'vocab_3'=2] {'vocab_0'}, dimensions={0}, use_global_device_ids=true | all-gather | bytes 40960 | tf_op jit(solution)/shard_map/all_gather | solution.py:18
  148.0 12.3 %all-gather.1 = f32[32,256]{1,0:T(8,128)S(1)} all-gather(f32[8,256]{1,0:T(8,128)S(1)} %pad_maximum_fusion.1), channel_id=3, replica_groups=mesh['vocab_0'=4,'vocab_1'=4,'vocab_2'=8,'vocab_3'=2] {'vocab_1'}, dimensions={0}, use_global_device_ids=true | all-gather | bytes 40960 | tf_op jit(solution)/shard_map/all_gather | solution.py:18
  160.3 24.6 %all-gather.2 = f32[64,256]{1,0:T(8,128)S(1)} all-gather(f32[8,256]{1,0:T(8,128)S(1)} %pad_maximum_fusion.2), channel_id=4, replica_groups=mesh['vocab_0'=4,'vocab_1'=4,'vocab_2'=8,'vocab_3'=2] {'vocab_2'}, dimensions={0}, use_global_device_ids=true | all-gather | bytes 73728 | tf_op jit(solution)/shard_map/all_gather | solution.py:18
  185.0 1.8 all-gather.3
  186.8 0.4 fusion.4
  187.2 0.1 dynamic-slice_subtract_fusion
  187.3 0.6 copy.22
  187.9 0.8 copy.19
  188.7 0.3 reshape.111
  189.0 7.7 %fusion.77 = f32[512,3584]{1,0:T(8,128)} fusion(bf16[512,768]{1,0:T(8,128)(2,1)S(1)} %reshape.111, bf16[3584,768]{1,0:T(8,128)(2,1)} %param.4), kind=kOutput, calls=%fused_computation.156 | convolution fusion | flops 2818572288 | bytes 13631488 | tf_op jit(solution)/shard_map/dot_general | solution.py:79
  196.7 141.2 %all-reduce.2 = bf16[512,3584]{1,0:T(8,128)(2,1)} all-reduce(f32[512,3584]{1,0:T(8,128)} %fusion.77), channel_id=6, replica_groups=mesh['vocab_0'=4,'vocab_1'=4,'vocab_2'=8,'vocab_3'=2] {'vocab_0','vocab_..., use_global_device_ids=true, to_apply=%region_4.5.clone | all-reduce | flops 1835008 | bytes 11010048
  337.9 2.4 copy.18
  340.3 1.6 convolution_convert_fusion
  341.9 4.1 %fusion = bf16[3584,768]{0,1:T(8,128)(2,1)} fusion(bf16[768,3584]{1,0:T(8,128)(2,1)S(1)} %convolution_convert_fusion, bf16[2,256,3584]{2,1,0:T(8,128)(2,1)S(1)} %copy.18, bf16[2,256,768]{2,1,0:T(8,128)(2,1)S(1)} %fusion.4), kind=kOutput, calls=%fused_computation.2 | convolution fusion | flops 1417543680 | bytes 13238272 | tf_op jit(solution)/shard_map/dot_general | solution.py:87
  345.9 8.3 %copy.23 = bf16[3584,768]{1,0:T(8,128)(2,1)} copy(bf16[3584,768]{0,1:T(8,128)(2,1)} %fusion) | data formatting | bytes 11010048
  354.2 1.4 fusion.5
  (12 shorter events, 0.2 us)
Async XLA Ops:
  7.2 121.3 %all-gather.6.cloned.1.call-start = ((), (), s32[]{:S(2)}) async-start(), calls=%async_computation | async-start | bytes 3684352 | tf_op jit(solution)/shard_map/all_gather | solution.py:66
  7.9 127.3 %copy-start = (bf16[2,256,768]{2,1,0:T(8,128)(2,1)S(1)}, bf16[2,256,768]{2,1,0:T(8,128)(2,1)}, u32[]{:S(2)}) copy-start(bf16[2,256,768]{2,1,0:T(8,128)(2,1)} %param.5) | copy-start | bytes 2359300
Sparse Core Ops, SparseCore 0:
  11.8 116.5 all-gather.5
where the time goes:
time: 363 us; the launch traced here: 362 us
  blocking collectives  192 us (53%)
  waiting for transfers between devices  121 us (33%)
  matrix products  20.1 us (6%)
  between operations  14.2 us (4%)
  local copies, waits for them, and re-layouts  13.8 us (4%)
    unnamed x1, blocking collectives  141 us
    all_gather x1, waiting for transfers between devices, shards(): shard_rows = lax.all_gather(hidden, VOCAB, axis=1, tiled=True)  121 us
    all_gather x4, blocking collectives, gathered_once(): both, at, found = (lax.all_gather(jnp.concatenate(lines), axis), 0, {})  50.6 us
    unnamed x4, local copies, waits for them, and re-layouts  8.87 us
    dot_general x1, matrix products, shards(): lax.dot_general(grad_block, head_weight, contract, preferred_element_type...  7.67 us
  transfers between devices with their start and end apart: 1, of which 1 were waited for; matrix products, arithmetic and copies ran while one was open for 0% of the time, Pallas kernels for 0%

commit v1 on v0

--- a/solution.py
+++ b/solution.py
@@ -63,7 +63,8 @@
 def shards(hidden, head_weight, teacher):
     group_count, row_count, model_width = hidden.shape
     contract = (((1,), (1,)), ((), ()))
-    shard_rows = lax.all_gather(hidden, VOCAB, axis=1, tiled=True)
+    outgoing = jnp.stack([hidden] * lax.axis_size(VOCAB))
+    shard_rows = jnp.concatenate(lax.all_to_all(outgoing, VOCAB, 0, 0), axis=1)
     logits = jnp.einsum("crd,dv->crv", shard_rows, head_weight, preferred_element_type=jnp.float32)
     token_loss, logit_grad = finish(logits, teacher)
     row_total = lax.axis_size(VOCAB) * (group_count * row_count)

time: 363 us -> 331 us (0.912)
  waiting for transfers between devices: 121 us -> 82 us
  starting transfers between devices: 0.04 us -> 15.5 us
  between operations: 14.2 us -> 0.77 us
  local copies, waits for them, and re-layouts: 13.8 us -> 18.2 us
    all_gather x1 -> x0, waiting for transfers between devices: 121 us -> none  [shards(): shard_rows = lax.all_gather(hidden, VOCAB, axis=1, tiled=True)]
    all_to_all x0 -> x1, waiting for transfers between devices: none -> 82 us  [shards(): shard_rows = jnp.concatenate(lax.all_to_all(outgoing, VOCAB, 0, 0), axis=1)]
    all_to_all x0 -> x1, starting transfers between devices: none -> 15.5 us  [shards(): shard_rows = jnp.concatenate(lax.all_to_all(outgoing, VOCAB, 0, 0), axis=1)]
    another operation x0 -> x1, local copies, waits for them, and re-layouts: none -> 4.44 us  [shards(): outgoing = jnp.stack([hidden] * lax.axis_size(VOCAB))]
where the time goes in v1:
time: 331 us; the launch traced here: 330 us
  blocking collectives  192 us (58%)
  waiting for transfers between devices  82 us (25%)
  matrix products  20.1 us (6%)
  local copies, waits for them, and re-layouts  18.2 us (5%)
  starting transfers between devices  15.5 us (5%)
    unnamed x1, blocking collectives  140 us
    all_to_all x1, waiting for transfers between devices, shards(): shard_rows = jnp.concatenate(lax.all_to_all(outgoing, VOCAB, 0, 0), axis=1)  82 us
    all_gather x4, blocking collectives, gathered_once(): both, at, found = (lax.all_gather(jnp.concatenate(lines), axis), 0, {})  52.2 us
    all_to_all x1, starting transfers between devices, shards(): shard_rows = jnp.concatenate(lax.all_to_all(outgoing, VOCAB, 0, 0), axis=1)  15.5 us
    unnamed x4, local copies, waits for them, and re-layouts  8.87 us
    dot_general x1, matrix products, shards(): lax.dot_general(grad_block, head_weight, contract, preferred_element_type...  7.67 us
    dot_general x1, matrix products, shards(): jnp.einsum('crd,dv->crv', shard_rows, head_weight, preferred_element_type...  6.76 us
  transfers between devices with their start and end apart: 1, of which 1 were waited for; matrix products, arithmetic and copies ran while one was open for 0% of the time, Pallas kernels for 0%

profile of v1, /device:TPU:0, one launch (start us, length us, event | category | flops | bytes accessed | tf_op | source)
XLA Modules:
  0.0 329.9 jit_solution(13470131108202146585)
XLA Ops:
  0.6 4.4 %stack.2 = bf16[256,2,1,3584]{3,1,2,0:T(2,128)(2,1)} broadcast(bf16[2,3584]{1,0:T(2,128)(2,1)} %bitcast.393), dimensions={1,3} | broadcast | bytes 3684352 | tf_op jit(solution)/shard_map/stack | solution.py:66
  5.1 15.5 %all-to-all-start = ((bf16[256,2,1,3584]{3,1,2,0:T(2,128)(2,1)}), bf16[256,2,1,3584]{3,1,2,0:T(2,128)(2,1)}, u32[]{:S(2)}, u32[]{:S(2)}) async-start(bf16[256,2,1,3584]{3,1,2,0:T(2,128)(2,1)} %stack.2), calls=%async_computation | async-start | bytes 7340032 | tf_op jit(solution)/shard_map/all_to_all | solution.py:67
  20.6 0.0 copy-start
  20.6 82.0 %all-to-all-done = bf16[256,2,1,3584]{3,1,2,0:T(2,128)(2,1)} async-done(((bf16[256,2,1,3584]{3,1,2,0:T(2,128)(2,1)}), bf16[256,2,1,3584]{3,1,2,0:T(2,128)(2,1)}, u32[]{:S(2)}, u32[]{:S(2)}) %all-to-all-start) | async-done | bytes 3670048 | tf_op jit(solution)/shard_map/all_to_all | solution.py:67
  102.6 6.8 %fusion.77 = (f32[2,256]{1,0:T(2,128)S(1)}, f32[2,256,768]{2,1,0:T(8,128)S(1)}) fusion(bf16[3584,768]{1,0:T(8,128)(2,1)} %param.4, bf16[256,2,1,3584]{3,1,2,0:T(2,128)(2,1)} %all-to-all-done), kind=kOutput, calls=%fused_computation.157 | convolution fusion | flops 2818964992 | bytes 10749952 | tf_op jit(solution)/shard_map/crd,dv->crv/dot_general | solution.py:68
  109.4 0.0 copy-done
  109.4 0.7 exponential_reduce_fusion
  110.1 11.9 %all-gather = f32[32,256]{1,0:T(8,128)S(1)} all-gather(f32[8,256]{1,0:T(8,128)S(1)} %pad_maximum_fusion), channel_id=2, replica_groups=mesh['vocab_0'=4,'vocab_1'=4,'vocab_2'=8,'vocab_3'=2] {'vocab_0'}, dimensions={0}, use_global_device_ids=true | all-gather | bytes 40960 | tf_op jit(solution)/shard_map/all_gather | solution.py:18
  122.1 12.5 %all-gather.1 = f32[32,256]{1,0:T(8,128)S(1)} all-gather(f32[8,256]{1,0:T(8,128)S(1)} %pad_maximum_fusion.1), channel_id=3, replica_groups=mesh['vocab_0'=4,'vocab_1'=4,'vocab_2'=8,'vocab_3'=2] {'vocab_1'}, dimensions={0}, use_global_device_ids=true | all-gather | bytes 40960 | tf_op jit(solution)/shard_map/all_gather | solution.py:18
  134.7 26.0 %all-gather.2 = f32[64,256]{1,0:T(8,128)S(1)} all-gather(f32[8,256]{1,0:T(8,128)S(1)} %pad_maximum_fusion.2), channel_id=4, replica_groups=mesh['vocab_0'=4,'vocab_1'=4,'vocab_2'=8,'vocab_3'=2] {'vocab_2'}, dimensions={0}, use_global_device_ids=true | all-gather | bytes 73728 | tf_op jit(solution)/shard_map/all_gather | solution.py:18
  160.7 1.8 all-gather.3
  162.5 0.4 fusion.6
  163.0 0.1 dynamic-slice_subtract_fusion
  163.0 0.6 copy.14
  163.6 0.8 copy.13
  164.5 0.3 reshape.126
  164.8 7.7 %fusion.78 = f32[512,3584]{1,0:T(8,128)} fusion(bf16[512,768]{1,0:T(8,128)(2,1)S(1)} %reshape.126, bf16[3584,768]{1,0:T(8,128)(2,1)} %param.4), kind=kOutput, calls=%fused_computation.158 | convolution fusion | flops 2818572288 | bytes 13631488 | tf_op jit(solution)/shard_map/dot_general | solution.py:80
  172.4 139.7 %all-reduce.2 = bf16[512,3584]{1,0:T(8,128)(2,1)} all-reduce(f32[512,3584]{1,0:T(8,128)} %fusion.78), channel_id=6, replica_groups=mesh['vocab_0'=4,'vocab_1'=4,'vocab_2'=8,'vocab_3'=2] {'vocab_0','vocab_..., use_global_device_ids=true, to_apply=%region_4.5.clone | all-reduce | flops 1835008 | bytes 11010048
  312.1 2.4 copy.23
  314.5 1.6 convolution_convert_fusion
  316.2 4.1 %fusion = bf16[3584,768]{0,1:T(8,128)(2,1)} fusion(bf16[768,3584]{1,0:T(8,128)(2,1)S(1)} %convolution_convert_fusion, bf16[2,256,1,3584]{3,1,0,2:T(8,128)(2,1)S(1)} %bitcast.383, bf16[2,256,768]{2,1,0:T(8,128)(2,1)S(1)} %fusion.6), kind=kOutput, calls=%fused_computation.2 | convolution fusion | flops 1417543680 | bytes 13238272 | tf_op jit(solution)/shard_map/dot_general | solution.py:88
  320.2 8.3 %copy.15 = bf16[3584,768]{1,0:T(8,128)(2,1)} copy(bf16[3584,768]{0,1:T(8,128)(2,1)} %fusion) | data formatting | bytes 11010048
  328.5 1.4 fusion.7
  (12 shorter events, 0.2 us)
Async XLA Ops:
  5.1 97.6 %all-to-all-start = ((bf16[256,2,1,3584]{3,1,2,0:T(2,128)(2,1)}), bf16[256,2,1,3584]{3,1,2,0:T(2,128)(2,1)}, u32[]{:S(2)}, u32[]{:S(2)}) async-start(bf16[256,2,1,3584]{3,1,2,0:T(2,128)(2,1)} %stack.2), calls=%async_computation | async-start | bytes 7340032 | tf_op jit(solution)/shard_map/all_to_all | solution.py:67
  20.6 88.8 %copy-start = (bf16[2,256,768]{2,1,0:T(8,128)(2,1)S(1)}, bf16[2,256,768]{2,1,0:T(8,128)(2,1)}, u32[]{:S(2)}) copy-start(bf16[2,256,768]{2,1,0:T(8,128)(2,1)} %param.5) | copy-start | bytes 2359300
